TPU v7x, 32 devices: a whole 2x2x4 slice. The times are simulated.
32 devices in a mesh: seq: 8 (over z, x), tp: 4 (over y, core).
Axes of the slice: x: 2, y: 2, z: 4, core: 2. Of those that a mesh axis runs over, the one named last changes fastest.
Arguments:
- queries: bfloat16 [1536, 6144], P('seq', 'tp'), may hold values from -400 to 400
- key_vectors: bfloat16 [1536, 1024], P('seq', 'tp'), may hold values from -8 to 8
- value_vectors: bfloat16 [1536, 1024], P('seq', 'tp'), may hold values from -6 to 6
- positions: int32 [1536], P('seq'), may hold values from 0 to 1535, as said below
- residual: bfloat16 [1536, 6144], P('seq', 'tp'), may hold values from -200 to 200
- norm_gain: float32 [1, 6144], P(None, 'tp'), may hold values from 0.5 to 1.5
- out_weight: bfloat16 [6144, 6144], P('tp'), may hold values from -0.3125 to 0.3125
Outputs:
- quantized: bfloat16 [1536, 6144], P('seq')
- token_scale: float32 [1536], P('seq')
- new_residual: bfloat16 [1536, 6144], P('seq', 'tp')
Inputs may be any that keep to these rules, and one draw needn't show every extreme that they name: The positions are a permutation of 0 to 1535. Cut into 16 runs of 96 consecutive positions, the rows of one index of seq hold run r in their first 96 rows and run 2 * 8 - 1 - r in their last ones, both in increasing order, with r differing between the indices of seq.
All inputs are finite; a program needn't handle non-finite values. Where the computation divides by a largest or mean magnitude, that divisor is 1e-20 or more.
Results may differ from a plain program's by a relative error of at most 0.012.
Values may be sent and summed in bfloat16 or wider, within the bound.
A program may use at most 64 MiB of HBM per device.

v0:
```python
import math

import jax
import jax.numpy as jnp
from jax import lax
from jax.sharding import PartitionSpec as P

D = 6144
Q_HEADS = 48
KV_HEADS = 8
HEAD = 128


NEG_FILL = -1e30


def fresh_state(kv_count, state_rows):
    return (
        jnp.full((kv_count, state_rows), NEG_FILL, jnp.float32),
        jnp.zeros((kv_count, state_rows), jnp.float32),
        jnp.zeros((kv_count, state_rows, HEAD), jnp.float32),
    )


def attend(state_now, query_part, half_rows_pos, key_block, value_block, key_pos):
    running_max, running_sum, weighted_sum = state_now
    kv_count = query_part.shape[0]
    group_size = Q_HEADS // KV_HEADS
    score_scale = 1.0 / math.sqrt(HEAD)
    query_pos = jnp.tile(half_rows_pos, group_size)
    key_heads = key_block.reshape(key_block.shape[0], kv_count, HEAD)
    value_heads = value_block.reshape(value_block.shape[0], kv_count, HEAD)
    scores = (
        jnp.einsum("kmd,skd->kms", query_part, key_heads, preferred_element_type=jnp.float32)
        * score_scale
    )
    visible = key_pos[None, :] <= query_pos[:, None]
    scores = jnp.where(visible[None], scores, NEG_FILL)
    new_max = jnp.maximum(running_max, jnp.max(scores, axis=2))
    weights = jnp.where(visible[None], jnp.exp(scores - new_max[..., None]), 0.0)
    factor = jnp.exp(running_max - new_max)
    running_sum = running_sum * factor + jnp.sum(weights, axis=2)
    weighted_sum = weighted_sum * factor[..., None] + jnp.einsum(
        "kms,skd->kmd",
        weights.astype(jnp.bfloat16),
        value_heads,
        preferred_element_type=jnp.float32,
    )
    return (new_max, running_sum, weighted_sum)


def fold_block(states, halves, half_pos, key_block, value_block, key_pos):
    result = []
    for half_index in range(2):

        def compute(state_now, half_index=half_index):
            return attend(
                state_now, halves[half_index], half_pos[half_index], key_block, value_block, key_pos
            )

        result.append(compute(states[half_index]))
    return tuple(result)


def fold_piece(states, halves, half_pos, key_piece, value_piece, key_pos):
    row_count = key_piece.shape[0]
    block_rows = math.gcd(row_count, 1024)
    block_count = row_count // block_rows

    def scan_step(loop_carry, block_pair):
        return (
            fold_block(loop_carry, halves, half_pos, block_pair[0], block_pair[1], block_pair[2]),
            None,
        )

    stacked = (
        key_piece.reshape(block_count, block_rows, key_piece.shape[1]),
        value_piece.reshape(block_count, block_rows, value_piece.shape[1]),
        key_pos.reshape(block_count, block_rows),
    )
    states, unused = lax.scan(scan_step, states, stacked)
    return states


def on_device(queries, key_vectors, value_vectors, positions, residual, norm_gain, out_weight):
    token_rows = queries.shape[0]
    run_rows = token_rows // 2
    group_size = Q_HEADS // KV_HEADS
    kv_count = key_vectors.shape[1] // HEAD
    query_split = queries.reshape(2, run_rows, kv_count, group_size, HEAD).transpose(0, 2, 3, 1, 4)
    query_split = query_split.reshape(2, kv_count, group_size * run_rows, HEAD)
    halves = (query_split[0], query_split[1])
    half_pos = (positions[:run_rows], positions[run_rows:])
    initial = (
        fresh_state(kv_count, group_size * run_rows),
        fresh_state(kv_count, group_size * run_rows),
    )
    all_pos = lax.all_gather(positions, "seq", axis=0, tiled=True)
    kv_pair = jnp.stack((key_vectors, value_vectors))
    pieces = lax.all_gather(kv_pair, "seq", axis=1, tiled=True)
    states = fold_piece(initial, halves, half_pos, pieces[0], pieces[1], all_pos)
    outputs = []
    for state_now in states:
        outputs.append((state_now[2] / state_now[1][..., None]).astype(jnp.bfloat16))
    attended = (
        jnp.stack(outputs).reshape(2, kv_count, group_size, run_rows, HEAD).transpose(0, 3, 1, 2, 4)
    )
    attended = attended.reshape(token_rows, kv_count * group_size * HEAD)
    partial_value = jnp.dot(attended, out_weight, preferred_element_type=jnp.float32)
    partial_value = partial_value.astype(jnp.bfloat16).astype(jnp.float32)
    summed = lax.psum_scatter(
        partial_value.astype(jnp.bfloat16), "tp", scatter_dimension=1, tiled=True
    ).astype(jnp.float32) + residual.astype(jnp.float32)
    square_sum = lax.psum(jnp.sum(summed * summed, axis=1), "tp")
    normed = summed * lax.rsqrt(square_sum / D + 1e-05)[:, None] * norm_gain
    peak_value = lax.pmax(jnp.max(jnp.abs(normed), axis=1), "tp") + 1e-06
    local_scaled = (normed / peak_value[:, None]).astype(jnp.bfloat16)
    quantized = lax.all_gather(local_scaled, "tp", axis=1, tiled=True)
    new_residual = summed.astype(jnp.bfloat16)
    return (quantized, peak_value, new_residual)


def solution(mesh):
    return jax.shard_map(
        on_device,
        mesh=mesh,
        in_specs=(
            P("seq", "tp"),
            P("seq", "tp"),
            P("seq", "tp"),
            P("seq"),
            P("seq", "tp"),
            P(None, "tp"),
            P("tp", None),
        ),
        out_specs=(P("seq", None), P("seq"), P("seq", "tp")),
        check_vma=False,
    )
```

profile of v0, /device:TPU:0, one launch (start us, length us, event | category | flops | bytes accessed | tf_op | source)
XLA Modules:
  0.0 205.4 jit_solution(1911410734703839984)
XLA Ops:
  7.2 1.6 pad_maximum_fusion
  9.0 1.8 reshape.108
  11.0 0.8 copy.22
  13.3 13.5 %all-reduce = s32[1536]{0:T(1024)S(1)} all-reduce(s32[1536]{0:T(1024)S(1)} %dynamic-update-slice), channel_id=1, replica_groups=mesh['seq'=8,'tp'=4] {'seq'}, use_global_device_ids=true, to_apply=%add | all-reduce | flops 1536 | bytes 12288
  28.1 29.7 %all-gather.3.cloned.1.call-done = bf16[2,1536,256]{2,1,0:T(8,128)(2,1)} async-done(((bf16[2,192,256]{2,1,0:T(8,128)(2,1)}), bf16[2,1536,256]{2,1,0:T(8,128)(2,1)}) %all-gather.3.cloned.1.call-update) | async-done | bytes 1572880 | tf_op jit(solution)/shard_map/all_gather | solution.py:100
  57.7 2.6 %fusion.27 = (bf16[1,1536,256]{2,1,0:T(8,128)(2,1)}, bf16[1,1536,256]{2,1,0:T(8,128)(2,1)}) fusion(bf16[2,1536,256]{2,1,0:T(8,128)(2,1)} %all-gather.3.cloned.1.call-done), kind=kLoop, calls=%fused_computation.56 | loop fusion | bytes 3145728 | tf_op jit(solution)/shard_map/slice | solution.py:101
  60.4 48.9 %while.21 = (s32[]{:T(128)}, f32[2,576]{1,0:T(2,128)S(1)}, f32[2,576]{1,0:T(2,128)S(1)}, f32[2,576,128]{2,1,0:T(8,128)}, f32[2,576]{1,0:T(2,128)S(1)}, /*index=5...) while((s32[]{:T(128)}, f32[2,576]{1,0:T(2,128)S(1)}, ...), condition=%wide.region_5.6_spmd.clone, body=%wide.region_0.5_spmd.clone.sunk | while | flops 620801280 | bytes 39185492 | solution.py:81
  60.4 0.7 constant_dynamic-slice_fusion.6
  62.9 1.0 constant_dynamic-slice_fusion.7
  64.8 1.0 fusion.66
  66.5 1.4 copy-done
  67.8 1.0 fusion.65
  69.4 1.0 constant_dynamic-slice_fusion.8
  70.4 0.8 copy.36
  71.2 3.5 %convolution_add_fusion.5 = f32[2,576,128]{2,1,0:T(8,128)} fusion(bf16[512,2,128]{0,2,1:T(8,128)(2,1)} %bitcast.79, f32[2,512,576]{1,2,0:T(8,128)} %copy-done, f32[2,576]{1,0:T(2,128)S(1)} %fusion.64, pred[576,512]{1,0:T(8,128)(4,1)S(1)} %get-tuple-element.288, f32[2,576,128]{2,1,0:T(8,128)} %get-tuple-element.318, ...), kind=kOutput, calls=%fused_computation.10.clone.1 | convolution fusion | flops 154386432 | bytes 4105217 | tf_op jit(solution)/shard_map/while/body/eval_jaxpr/kms,skd->kmd/dot_general | solution.py:43
  74.7 1.0 convolution_add_fusion.4
  75.7 0.8 copy-done.6
  76.5 0.7 constant_dynamic-slice_fusion.6
  79.1 1.0 constant_dynamic-slice_fusion.7
  80.9 1.0 fusion.66
  81.9 0.7 fusion.63
  82.6 1.4 copy-done
  84.0 1.0 fusion.65
  85.6 1.0 constant_dynamic-slice_fusion.8
  86.6 0.8 copy.36
  87.4 3.7 %convolution_add_fusion.5 = f32[2,576,128]{2,1,0:T(8,128)} fusion(bf16[512,2,128]{0,2,1:T(8,128)(2,1)} %bitcast.79, f32[2,512,576]{1,2,0:T(8,128)} %copy-done, f32[2,576]{1,0:T(2,128)S(1)} %fusion.64, pred[576,512]{1,0:T(8,128)(4,1)S(1)} %get-tuple-element.288, f32[2,576,128]{2,1,0:T(8,128)} %get-tuple-element.318, ...), kind=kOutput, calls=%fused_computation.10.clone.1 | convolution fusion | flops 154386432 | bytes 4105217 | tf_op jit(solution)/shard_map/while/body/eval_jaxpr/kms,skd->kmd/dot_general | solution.py:43
  91.1 1.0 convolution_add_fusion.4
  92.1 0.8 copy-done.6
  92.9 0.7 constant_dynamic-slice_fusion.6
  95.5 1.0 constant_dynamic-slice_fusion.7
  97.3 1.0 fusion.66
  99.0 1.4 copy-done
  100.4 1.0 fusion.65
  102.0 1.0 constant_dynamic-slice_fusion.8
  102.9 0.8 copy.36
  103.8 3.7 %convolution_add_fusion.5 = f32[2,576,128]{2,1,0:T(8,128)} fusion(bf16[512,2,128]{0,2,1:T(8,128)(2,1)} %bitcast.79, f32[2,512,576]{1,2,0:T(8,128)} %copy-done, f32[2,576]{1,0:T(2,128)S(1)} %fusion.64, pred[576,512]{1,0:T(8,128)(4,1)S(1)} %get-tuple-element.288, f32[2,576,128]{2,1,0:T(8,128)} %get-tuple-element.318, ...), kind=kOutput, calls=%fused_computation.10.clone.1 | convolution fusion | flops 154386432 | bytes 4105217 | tf_op jit(solution)/shard_map/while/body/eval_jaxpr/kms,skd->kmd/dot_general | solution.py:43
  107.4 1.0 convolution_add_fusion.4
  108.4 0.8 copy-done.6
  109.2 1.6 divide_convert_fusion.1
  112.0 11.6 %convolution_convert_fusion = bf16[192,6144]{1,0:T(8,128)(2,1)} fusion(bf16[192,1536]{1,0:T(8,128)(2,1)S(1)} %reshape.109, bf16[1536,6144]{1,0:T(8,128)(2,1)} %param.15), kind=kOutput, calls=%fused_computation.43 | convolution fusion | flops 3625058304 | bytes 21823488 | tf_op jit(solution)/shard_map/dot_general | solution.py:109
  124.3 30.6 %reduce-scatter.2.cloned.1.call-done = bf16[192,1536]{1,0:T(8,128)(2,1)} async-done(((bf16[192,6144]{1,0:T(8,128)(2,1)}), bf16[192,1536]{1,0:T(8,128)(2,1)}) %reduce-scatter.2.cloned.1.call-update) | async-done | bytes 589840 | tf_op jit(solution)/shard_map/reduce_scatter | solution.py:111
  154.9 1.4 multiply_reduce_fusion
  156.3 5.8 %psum.7 = f32[192]{0:T(256)S(1)} all-reduce(f32[192]{0:T(256)S(1)} %multiply_reduce_fusion), channel_id=1, replica_groups=mesh['seq'=8,'tp'=4] {'tp'}, use_global_device_ids=true, to_apply=%region_8.9 | all-reduce | flops 192 | bytes 1536 | tf_op jit(solution)/shard_map/psum | solution.py:114
  162.1 1.4 abs_reduce_fusion
  163.5 5.7 %pmax.7 = f32[192]{0:T(256)S(1)} all-reduce(f32[192]{0:T(256)S(1)} %abs_reduce_fusion), channel_id=1, replica_groups=mesh['seq'=8,'tp'=4] {'tp'}, use_global_device_ids=true, to_apply=%region_10.11 | all-reduce | flops 192 | bytes 1536 | tf_op jit(solution)/shard_map/pmax | solution.py:116
  169.2 1.3 fusion.26
  170.5 25.0 %all-gather.5.cloned.1.call-done = bf16[192,6144]{1,0:T(8,128)(2,1)} async-done(((bf16[192,1536]{1,0:T(8,128)(2,1)}), bf16[192,6144]{1,0:T(8,128)(2,1)}) %all-gather.5.cloned.1.call-update) | async-done | bytes 2359312 | tf_op jit(solution)/shard_map/all_gather | solution.py:118
  195.5 3.3 %copy.60 = bf16[192,6144]{1,0:T(8,128)(2,1)} copy(bf16[192,6144]{1,0:T(8,128)(2,1)} %all-gather.5.cloned.1.call-done) | data formatting | bytes 4718592
  (106 shorter events, 15.7 us)
Async XLA Ops:
  7.2 50.6 %all-gather.3.cloned.1.call-start = ((), (), s32[]{:S(2)}) async-start(), calls=%async_computation.1 | async-start | bytes 1769472 | tf_op jit(solution)/shard_map/all_gather | solution.py:100
  8.8 2.9 %copy-start.11 = (u32[32]{0:T(128)S(1)}, u32[32]{0:T(128)}, u32[]{:S(2)}) copy-start(u32[32]{0:T(128)} %constant.37) | copy-start | bytes 388
  8.9 4.2 %copy-start.10 = (s32[192]{0:T(256)S(1)}, s32[192]{0:T(256)}, u32[]{:S(2)}) copy-start(s32[192]{0:T(256)} %param.12) | copy-start | bytes 2308
  8.9 146.0 %reduce-scatter.2.cloned.1.call-start = ((), (), s32[]{:S(2)}) async-start(), calls=%async_computation.2 | async-start | bytes 2949120 | tf_op jit(solution)/shard_map/reduce_scatter | solution.py:111
  64.8 1.0 copy-start.1
  66.4 1.4 copy-start
  71.2 3.5 %copy-start.2 = (bf16[1,512,256]{1,2,0:T(8,128)(2,1)S(1)}, bf16[1,512,256]{1,2,0:T(8,128)(2,1)}, u32[]{:S(2)}) copy-start(bf16[1,512,256]{1,2,0:T(8,128)(2,1)} %copy.36) | copy-start | bytes 786436 | tf_op jit(solution)/shard_map/while
  71.2 3.5 %copy-start.5 = (f32[2,576,128]{2,1,0:T(8,128)S(1)}, f32[2,576,128]{2,1,0:T(8,128)}, u32[]{:S(2)}) copy-start(f32[2,576,128]{2,1,0:T(8,128)} %get-tuple-element.315) | copy-start | bytes 1769476 | tf_op jit(solution)/shard_map/while
  71.2 3.5 %copy-start.7 = (f32[2,576]{1,0:T(2,128)S(1)}, f32[2,576]{1,0:T(2,128)}, u32[]{:S(2)}) copy-start(f32[2,576]{1,0:T(2,128)} %get-tuple-element.293) | copy-start | bytes 13828 | tf_op jit(solution)/shard_map/while
  75.7 0.8 copy-start.6
  80.9 1.0 copy-start.1
  82.6 1.4 copy-start
  87.4 3.7 %copy-start.2 = (bf16[1,512,256]{1,2,0:T(8,128)(2,1)S(1)}, bf16[1,512,256]{1,2,0:T(8,128)(2,1)}, u32[]{:S(2)}) copy-start(bf16[1,512,256]{1,2,0:T(8,128)(2,1)} %copy.36) | copy-start | bytes 786436 | tf_op jit(solution)/shard_map/while
  87.4 3.7 %copy-start.5 = (f32[2,576,128]{2,1,0:T(8,128)S(1)}, f32[2,576,128]{2,1,0:T(8,128)}, u32[]{:S(2)}) copy-start(f32[2,576,128]{2,1,0:T(8,128)} %get-tuple-element.315) | copy-start | bytes 1769476 | tf_op jit(solution)/shard_map/while
  87.4 3.7 %copy-start.7 = (f32[2,576]{1,0:T(2,128)S(1)}, f32[2,576]{1,0:T(2,128)}, u32[]{:S(2)}) copy-start(f32[2,576]{1,0:T(2,128)} %get-tuple-element.293) | copy-start | bytes 13828 | tf_op jit(solution)/shard_map/while
  92.1 0.8 copy-start.6
  97.3 1.0 copy-start.1
  98.9 1.4 copy-start
  103.8 3.7 %copy-start.2 = (bf16[1,512,256]{1,2,0:T(8,128)(2,1)S(1)}, bf16[1,512,256]{1,2,0:T(8,128)(2,1)}, u32[]{:S(2)}) copy-start(bf16[1,512,256]{1,2,0:T(8,128)(2,1)} %copy.36) | copy-start | bytes 786436 | tf_op jit(solution)/shard_map/while
  103.8 3.7 %copy-start.5 = (f32[2,576,128]{2,1,0:T(8,128)S(1)}, f32[2,576,128]{2,1,0:T(8,128)}, u32[]{:S(2)}) copy-start(f32[2,576,128]{2,1,0:T(8,128)} %get-tuple-element.315) | copy-start | bytes 1769476 | tf_op jit(solution)/shard_map/while
  103.8 3.7 %copy-start.7 = (f32[2,576]{1,0:T(2,128)S(1)}, f32[2,576]{1,0:T(2,128)}, u32[]{:S(2)}) copy-start(f32[2,576]{1,0:T(2,128)} %get-tuple-element.293) | copy-start | bytes 13828 | tf_op jit(solution)/shard_map/while
  108.4 0.8 copy-start.6
  123.6 0.7 copy-start.8
  123.6 31.3 %copy-start.3 = (bf16[192,1536]{1,0:T(8,128)(2,1)S(1)}, bf16[192,1536]{1,0:T(8,128)(2,1)}, u32[]{:S(2)}) copy-start(bf16[192,1536]{1,0:T(8,128)(2,1)} %param.13) | copy-start | bytes 1769476
  123.6 71.9 %all-gather.5.cloned.1.call-start = ((), (), s32[]{:S(2)}) async-start(), calls=%async_computation.3 | async-start | bytes 2949120 | tf_op jit(solution)/shard_map/all_gather | solution.py:118
  154.9 14.3 %copy-start.4 = (bf16[192,1536]{1,0:T(8,128)(2,1)S(1)}, bf16[192,1536]{1,0:T(8,128)(2,1)}, u32[]{:S(2)}) copy-start(bf16[192,1536]{1,0:T(8,128)(2,1)} %reduce-scatter.2.cloned.1.call-done) | copy-start | bytes 1769476
  169.2 29.7 %copy-start.9 = (f32[192]{0:T(256)}, f32[192]{0:T(256)S(1)}, u32[]{:S(2)}) copy-start(f32[192]{0:T(256)S(1)} %broadcast_add_fusion) | copy-start | bytes 2308
Sparse Core Ops, SparseCore 0:
  10.7 46.9 all-gather.2
  123.7 31.1 reduce-scatter.1
  170.6 24.8 all-gather.4
where the time goes:
time: 206 us; the launch traced here: 205 us
  waiting for transfers between devices  85.3 us (41%)
  local copies, waits for them, and re-layouts  34.3 us (17%)
  matrix products  29.4 us (14%)
  blocking collectives  24.9 us (12%)
  other arithmetic  16.5 us (8%)
  between operations  14.5 us (7%)
    reduce_scatter x1, waiting for transfers between devices, on_device(): lax.psum_scatter(partial_value.astype(jnp.bfloat16), 'tp', scatter_dimens...  30.6 us
    all_gather x1, waiting for transfers between devices, on_device(): pieces = lax.all_gather(kv_pair, 'seq', axis=1, tiled=True)  29.7 us
    all_gather x1, waiting for transfers between devices, on_device(): quantized = lax.all_gather(local_scaled, 'tp', axis=1, tiled=True)  25 us
    dot_general x6, matrix products, attend(): jnp.einsum('kms,skd->kmd', weights.astype(jnp.bfloat16), value_heads, pre...  13.7 us
    unnamed x1, blocking collectives  13.5 us
    dot_general x1, matrix products, on_device(): jnp.dot(attended, out_weight, preferred_element_type=jnp.float32)  11.6 us
    dynamic_slice x15, local copies, waits for them, and re-layouts, fold_piece(): states, unused = lax.scan(scan_step, states, stacked)  10.9 us
    while x42, local copies, waits for them, and re-layouts  6.63 us
  transfers between devices with their start and end apart: 3, of which 3 were waited for; matrix products, arithmetic and copies ran while one was open for 2% of the time, Pallas kernels for 0%

commit v1 on v0

v1 whole, which is shorter than its diff:
```python
import functools
import math

import jax
import jax.numpy as jnp
from jax import lax
from jax.experimental import pallas as pl
from jax.experimental.pallas import tpu as pltpu
from jax.sharding import PartitionSpec as P

HEAD = 128
LOG2E = 1.4426950408889634
MASKED = -1e30
MESH = pl.DeviceIdType.MESH
F32 = jnp.float32
BF16 = jnp.bfloat16


def kernel(
    dims,
    pos_ref, key_ref, value_ref, gain_ref, query_hbm, residual_hbm, weight_hbm,
    quant_hbm, scale_hbm, stream_hbm,
    kv, pos_all, gain_all, query_raw, residual_raw, query, residual, weight,
    attended, part, from_core, pair, gained, quant, stream, scale,
    load_sem, kv_send, kv_recv, forward_send, pos_send, pos_recv, gain_send, gain_recv,
    core_send, core_recv, y_send, y_recv, out_send, out_recv, out_local,
):
    n_seq, n_tp, group, kv_count, half, tile = dims
    n_y = n_tp // 2
    me = lax.axis_index("seq")
    tp = lax.axis_index("tp")
    core = lax.rem(tp, 2)
    y = tp // 2
    core_peer = tp + 1 - 2 * core
    partner = me + 1 - 2 * lax.rem(me, 2)
    model = weight.shape[1]
    tiles = model // tile
    slice_width = model // n_tp
    tiles_slice = slice_width // tile
    own = half // 2
    keys = n_seq * half

    loads = [
        pltpu.make_async_copy(query_hbm, query_raw, load_sem.at[0]),
        pltpu.make_async_copy(residual_hbm, residual_raw, load_sem.at[1]),
        pltpu.make_async_copy(weight_hbm, weight, load_sem.at[2]),
    ]
    for load in loads:
        load.start()

    barrier = pltpu.get_barrier_semaphore()
    for step in range(1, n_seq):
        pl.semaphore_signal(
            barrier, inc=1, device_id=(lax.rem(me + step, n_seq), tp), device_id_type=MESH
        )
    for step in range(1, n_tp):
        pl.semaphore_signal(
            barrier, inc=1, device_id=(me, lax.rem(tp + step, n_tp)), device_id_type=MESH
        )

    first = pos_ref[0:1, 0:1].astype(F32)
    second = pos_ref[0:1, half : half + 1].astype(F32)
    keep = jnp.where(first < second, 1.0, 0.0)

    def split(ref):
        top = ref[:half, :].astype(F32)
        bottom = ref[half:, :].astype(F32)
        low = top * keep + bottom * (1.0 - keep)
        high = bottom * keep + top * (1.0 - keep)
        return low.astype(BF16), high.astype(BF16)

    for index, ref in enumerate((key_ref, value_ref)):
        low, high = split(ref)
        kv[0, me, index] = low
        kv[1, me, index] = high
    pos_all[me] = pos_ref[...]
    gain_all[tp] = gain_ref[...]
    pl.semaphore_wait(barrier, n_seq + n_tp - 2)

    line = n_seq // 2
    order = []
    for step in range(1, line // 2 + 1):
        order.append(step)
        if line - step != step:
            order.append(line - step)
    sent = []

    def remote(src, dst, send, recv, device):
        copy = pltpu.make_async_remote_copy(
            src_ref=src, dst_ref=dst, send_sem=send, recv_sem=recv,
            device_id=device, device_id_type=MESH,
        )
        copy.start()
        sent.append(copy)
        return copy

    def landed(dst, recv):
        pltpu.make_async_remote_copy(
            src_ref=dst, dst_ref=dst, send_sem=recv, recv_sem=recv,
            device_id=(partner, tp), device_id_type=MESH,
        ).wait_recv()

    def send_line(phase):
        for step in order:
            target = lax.rem(me + 2 * step, n_seq)
            remote(
                kv.at[phase, me], kv.at[phase, me], kv_send.at[phase, step],
                kv_recv.at[phase, me], (target, tp),
            )

    def send_partner(phase):
        remote(
            kv.at[phase, me], kv.at[phase, me], kv_send.at[phase, 0],
            kv_recv.at[phase, me], (partner, tp),
        )

    def forward(phase, step):
        source = lax.rem(me + 2 * step, n_seq)
        landed(kv.at[phase, source], kv_recv.at[phase, source])
        remote(
            kv.at[phase, source], kv.at[phase, source], forward_send.at[phase, step],
            kv_recv.at[phase, source], (partner, tp),
        )

    def arrivals(phase):
        for step in range(line):
            source = lax.rem(partner + 2 * step, n_seq)
            landed(kv.at[phase, source], kv_recv.at[phase, source])

    send_partner(0)
    send_line(0)
    for step in range(1, n_seq):
        remote(
            pos_ref, pos_all.at[me], pos_send.at[step], pos_recv.at[me],
            (lax.rem(me + step, n_seq), tp),
        )
    for step in range(1, n_tp):
        remote(
            gain_ref, gain_all.at[tp], gain_send.at[step], gain_recv.at[tp],
            (me, lax.rem(tp + step, n_tp)),
        )
    loads[0].wait()
    loads[1].wait()
    query[0], query[1] = split(query_raw)
    residual[0], residual[1] = split(residual_raw)
    for step in order:
        forward(0, step)
    send_line(1)
    send_partner(1)
    for step in range(1, n_seq):
        source = lax.rem(me + step, n_seq)
        landed(pos_all.at[source], pos_recv.at[source])
    arrivals(0)

    lanes = lax.broadcasted_iota(jnp.int32, (1, keys), 1)
    rows = lax.broadcasted_iota(jnp.int32, (half, 1), 0).astype(F32)

    def bias(phase):
        pick = jnp.minimum if phase == 0 else jnp.maximum

        def base(index):
            value = pos_all[index]
            return pick(value[0:1, 0:1].astype(F32), value[0:1, half : half + 1].astype(F32))

        key_pos = jnp.zeros((1, keys), F32)
        for source in range(n_seq):
            inside = (lanes >= source * half) & (lanes < (source + 1) * half)
            key_pos = jnp.where(
                inside, base(source) + (lanes - source * half).astype(F32), key_pos
            )
        return jnp.where(key_pos <= base(me) + rows, 0.0, MASKED)

    stack = group if keys <= 1024 else 1

    def attend(phase):
        mask = bias(phase)
        for head in range(0, kv_count * group, stack):
            kv_head = head // group
            columns = slice(kv_head * HEAD, (kv_head + 1) * HEAD)
            block = jnp.concatenate(
                [
                    query[phase, :, (head + i) * HEAD : (head + i + 1) * HEAD]
                    for i in range(stack)
                ],
                axis=0,
            )
            scores = []
            for piece in range(phase + 1):
                key_rows = kv[piece, :, 0, :, columns].reshape(keys, HEAD)
                value = lax.dot_general(
                    block, key_rows, (((1,), (1,)), ((), ())), preferred_element_type=F32
                ).reshape(stack, half, keys)
                scores.append(value + mask[None] if piece == phase else value)
            peak = jnp.max(scores[0], axis=2, keepdims=True)
            for value in scores[1:]:
                peak = jnp.maximum(peak, jnp.max(value, axis=2, keepdims=True))
            mixed = jnp.zeros((stack * half, HEAD), F32)
            total = jnp.zeros((stack, half, 1), F32)
            for piece, value in enumerate(scores):
                weights = jnp.exp2((value - peak) * (LOG2E / math.sqrt(HEAD)))
                total += jnp.sum(weights, axis=2, keepdims=True)
                value_rows = kv[piece, :, 1, :, columns].reshape(keys, HEAD)
                mixed += jnp.dot(
                    weights.astype(BF16).reshape(stack * half, keys), value_rows,
                    preferred_element_type=F32,
                )
            mixed = (mixed.reshape(stack, half, HEAD) / total).astype(BF16)
            for i in range(stack):
                attended[phase, :, (head + i) * HEAD : (head + i + 1) * HEAD] = mixed[i]

    def reduce_tile(phase, index):
        landed(from_core.at[phase, index], core_recv.at[phase, index])
        both = part[phase, index, core].astype(F32) + from_core[phase, index].astype(F32)
        pair[phase, y, index] = both.astype(BF16)
        for step in range(1, n_y):
            target = lax.rem(y + step, n_y) * 2 + core
            remote(
                pair.at[phase, y, index], pair.at[phase, y, index],
                y_send.at[phase, index, step], y_recv.at[phase, y, index], (me, target),
            )

    def project(phase, between):
        for index in range(tiles):
            columns = slice(index * tile, (index + 1) * tile)
            product = jnp.dot(
                attended[phase], weight[:, columns], preferred_element_type=F32
            )
            inner = (index % tiles_slice) * tile
            mine = jnp.where(tp == index // tiles_slice, 1.0, 0.0)
            product += residual[phase, :, inner : inner + tile].astype(F32) * mine
            part[phase, index] = product.astype(BF16).reshape(2, own, tile)
            remote(
                part.at[phase, index, 1 - core], from_core.at[phase, index],
                core_send.at[phase, index], core_recv.at[phase, index], (me, core_peer),
            )
            if index >= 1:
                reduce_tile(phase, index - 1)
            if index < len(between):
                between[index]()
        reduce_tile(phase, tiles - 1)
        for task in between[tiles:]:
            task()

    locals_out = []

    def finish(phase):
        square = jnp.zeros((own, 1), F32)
        peak = jnp.zeros((own, 1), F32)
        for index in range(tiles):
            for step in range(1, n_y):
                source = lax.rem(y + step, n_y)
                landed(pair.at[phase, source, index], y_recv.at[phase, source, index])
            total = pair[phase, 0, index].astype(F32)
            for source in range(1, n_y):
                total += pair[phase, source, index].astype(F32)
            inner = (index % tiles_slice) * tile
            stream[phase, index // tiles_slice, :, inner : inner + tile] = total.astype(BF16)
            square += jnp.sum(total * total, axis=1, keepdims=True)
            scaled = total * gain_all[index // tiles_slice, :, inner : inner + tile]
            gained[index] = scaled
            peak = jnp.maximum(peak, jnp.max(jnp.abs(scaled), axis=1, keepdims=True))
        inverse = lax.rsqrt(square / model + 1e-5)
        token = inverse * peak + 1e-6
        factor = inverse / token
        scale[phase] = jnp.broadcast_to(token, (own, 128))
        for index in range(tiles):
            quant[phase, :, index * tile : (index + 1) * tile] = (gained[index] * factor).astype(
                BF16
            )
        sends = (
            (quant.at[phase], quant.at[phase], quant_hbm),
            (stream.at[phase, tp], stream.at[phase, core_peer], stream_hbm),
            (scale.at[phase], scale.at[phase], scale_hbm),
        )
        for index, (here, there, out) in enumerate(sends):
            remote(
                there, out.at[phase, core], out_send.at[phase, index],
                out_recv.at[phase, index], (me, core_peer),
            )
            copy = pltpu.make_async_copy(here, out.at[phase, core], out_local.at[phase, index])
            copy.start()
            locals_out.append(copy)

    attend(0)
    loads[2].wait()
    project(0, [functools.partial(forward, 1, step) for step in order])
    arrivals(1)
    attend(1)
    project(1, [])
    for step in range(1, n_tp):
        source = lax.rem(tp + step, n_tp)
        landed(gain_all.at[source], gain_recv.at[source])
    finish(0)
    finish(1)
    for phase in range(2):
        for index, out in enumerate((quant_hbm, stream_hbm, scale_hbm)):
            landed(out.at[phase, 1 - core], out_recv.at[phase, index])
    for copy in locals_out:
        copy.wait()
    for copy in sent:
        copy.wait_send()


def on_device(n_seq, n_tp, queries, key_vectors, value_vectors, positions, residual, norm_gain, out_weight):
    token_rows, query_width = queries.shape
    half = token_rows // 2
    own = half // 2
    kv_width = key_vectors.shape[1]
    kv_count = kv_width // HEAD
    group = query_width // kv_width
    model = out_weight.shape[1]
    slice_width = residual.shape[1]
    tile = math.gcd(slice_width, 768)
    tiles = model // tile
    n_y = n_tp // 2
    vmem = pl.BlockSpec(memory_space=pltpu.VMEM)
    anywhere = pl.BlockSpec(memory_space=pl.ANY)
    dma = pltpu.SemaphoreType.DMA
    line = n_seq // 2
    quant, scale, stream = pl.pallas_call(
        functools.partial(kernel, (n_seq, n_tp, group, kv_count, half, tile)),
        out_shape=(
            jax.ShapeDtypeStruct((2, 2, own, model), BF16),
            jax.ShapeDtypeStruct((2, 2, own, 128), F32),
            jax.ShapeDtypeStruct((2, 2, own, slice_width), BF16),
        ),
        in_specs=[vmem, vmem, vmem, vmem, anywhere, anywhere, anywhere],
        out_specs=(anywhere, anywhere, anywhere),
        scratch_shapes=[
            pltpu.VMEM((2, n_seq, 2, half, kv_width), BF16),
            pltpu.VMEM((n_seq, 1, token_rows), jnp.int32),
            pltpu.VMEM((n_tp, 1, slice_width), F32),
            pltpu.VMEM(queries.shape, BF16),
            pltpu.VMEM(residual.shape, BF16),
            pltpu.VMEM((2, half, query_width), BF16),
            pltpu.VMEM((2, half, slice_width), BF16),
            pltpu.VMEM(out_weight.shape, BF16),
            pltpu.VMEM((2, half, query_width), BF16),
            pltpu.VMEM((2, tiles, 2, own, tile), BF16),
            pltpu.VMEM((2, tiles, own, tile), BF16),
            pltpu.VMEM((2, n_y, tiles, own, tile), BF16),
            pltpu.VMEM((tiles, own, tile), F32),
            pltpu.VMEM((2, own, model), BF16),
            pltpu.VMEM((2, n_tp, own, slice_width), BF16),
            pltpu.VMEM((2, own, 128), F32),
            dma((3,)),
            dma((2, line)),
            dma((2, n_seq)),
            dma((2, line)),
            dma((n_seq,)),
            dma((n_seq,)),
            dma((n_tp,)),
            dma((n_tp,)),
            dma((2, tiles)),
            dma((2, tiles)),
            dma((2, tiles, n_y)),
            dma((2, n_y, tiles)),
            dma((2, 3)),
            dma((2, 3)),
            dma((2, 3)),
        ],
        compiler_params=pltpu.CompilerParams(
            collective_id=0, has_side_effects=True, vmem_limit_bytes=63 * 1024 * 1024
        ),
    )(positions[None, :], key_vectors, value_vectors, norm_gain, queries, residual, out_weight)
    ordered = positions[0] < positions[half]

    def restore(value):
        top = jnp.where(ordered, value[0], value[1])
        bottom = jnp.where(ordered, value[1], value[0])
        return jnp.stack((top, bottom)).reshape((token_rows,) + value.shape[3:])

    return (restore(quant), restore(scale[..., 0]), restore(stream))


def solution(mesh):
    return jax.shard_map(
        functools.partial(on_device, mesh.shape["seq"], mesh.shape["tp"]),
        mesh=mesh,
        in_specs=(
            P("seq", "tp"),
            P("seq", "tp"),
            P("seq", "tp"),
            P("seq"),
            P("seq", "tp"),
            P(None, "tp"),
            P("tp", None),
        ),
        out_specs=(P("seq", None), P("seq"), P("seq", "tp")),
        check_vma=False,
    )
```

time: 206 us -> 64.2 us (0.31)
  waiting for transfers between devices: 85.3 us -> 0 us
  Pallas kernels: 0 us -> 55.6 us
  local copies, waits for them, and re-layouts: 34.3 us -> 1.99 us
  matrix products: 29.4 us -> 0 us
  blocking collectives: 24.9 us -> 0 us
  between operations: 14.5 us -> 1.98 us
  other arithmetic: 16.5 us -> 4.41 us
    pallas_call x0 -> x1, Pallas kernels: none -> 55.6 us  [on_device(): pl.pallas_call(functools.partial(kernel, (n_seq, n_tp, group, kv_count, h...]
    all_gather x2 -> x0, waiting for transfers between devices: 54.7 us -> none  [the longest x1 29.7 us: on_device(): pieces = lax.all_gather(kv_pair, 'seq', axis=1, tiled=True)]
    reduce_scatter x1 -> x0, waiting for transfers between devices: 30.6 us -> none  [on_device(): lax.psum_scatter(partial_value.astype(jnp.bfloat16), 'tp', scatter_dimens...]
    dot_general x13 -> x0, matrix products: 29.4 us -> none  [the longest x6 13.7 us: attend(): jnp.einsum('kms,skd->kmd', weights.astype(jnp.bfloat16), value_heads, pre...]
    unnamed x1 -> x0, blocking collectives: 13.5 us -> none
    dynamic_slice x15 -> x0, local copies, waits for them, and re-layouts: 10.9 us -> none  [fold_piece(): states, unused = lax.scan(scan_step, states, stacked)]
    reduce_sum x7 -> x0, other arithmetic: 7.25 us -> none  [the longest x6 5.84 us: attend(): running_sum = running_sum * factor + jnp.sum(weights, axis=2)]
    while x42 -> x0, local copies, waits for them, and re-layouts: 6.63 us -> none
  transfers between devices with their start and end apart: 3 -> 0, of which waited for: 3 -> 0; matrix products, arithmetic and copies ran while one was open for 2% -> 0% of each run, Pallas kernels for 0% -> 0%
where the time goes in v1:
time: 64.2 us; the launch traced here: 63.9 us
  Pallas kernels  55.6 us (87%)
  other arithmetic  4.41 us (7%)
  local copies, waits for them, and re-layouts  1.99 us (3%)
  between operations  1.98 us (3%)
    pallas_call x1, Pallas kernels, on_device(): pl.pallas_call(functools.partial(kernel, (n_seq, n_tp, group, kv_count, h...  55.6 us
    another operation x3, other arithmetic, restore(): return jnp.stack((top, bottom)).reshape((token_rows,) + value.shape[3:])  2.48 us
    select_n x3, other arithmetic, restore(): top = jnp.where(ordered, value[0], value[1])  1.93 us
    slice x1, local copies, waits for them, and re-layouts, on_device(): ordered = positions[0] < positions[half]  1.34 us

profile of v1, /device:TPU:0, one launch (start us, length us, event | category | flops | bytes accessed | tf_op | source)
XLA Modules:
  0.0 63.9 jit_solution(15224266114363438780)
XLA Ops:
  0.6 1.3 %fusion = (s32[1]{0:T(128)}, s32[1]{0:T(128)}) fusion(s32[192]{0:T(256)} %param.10), kind=kLoop, calls=%fused_computation.9 | loop fusion | bytes 16 | tf_op jit(solution)/shard_map/slice | solution.py:366
  3.3 55.6 %shard_map.94 = (bf16[2,2,48,6144]{3,2,1,0:T(8,128)(2,1)}, f32[2,2,48,128]{3,2,1,0:T(8,128)}, bf16[2,2,48,1536]{3,2,1,0:T(8,128)(2,1)}) custom-call(s32[1,192]{1,0:T(1,128)} %bitcast.8, bf16[192,256]{1,0:T(8,128)(2,1)} %key_ref.1, bf16[192,256]{1,0:T(8,128)(2,1)} %value_ref.1, f32[1,1536]{1,0:T(1,128)} %gain_ref.1, bf16[192,1536]{1,0:T(8,128)(2,1)} %query_hbm.1, ...), custom_call_target="tpu_custom_call" | custom-call | tf_op jit(solution)/shard_map/pallas_call | solution.py:320
  58.8 1.8 %broadcast_select_fusion.1 = (bf16[1,2,48,6144]{3,2,1,0:T(8,128)(2,1)S(1)}, bf16[1,2,48,6144]{3,2,1,0:T(8,128)(2,1)S(1)}) fusion(pred[]{:T(512)} %bitcast, bf16[2,2,48,6144]{3,2,1,0:T(8,128)(2,1)} %get-tuple-element.6), kind=kLoop, calls=%fused_computation.2 | loop fusion | flops 1179648 | bytes 4718593 | tf_op jit(solution)/shard_map/jit(_where)/select_n | solution.py:369
  60.6 0.0 copy-start.1
  60.6 0.0 copy-start
  60.6 1.6 %pad_maximum_fusion = bf16[2,2,48,6144]{3,2,1,0:T(8,128)(2,1)} fusion(bf16[1,2,48,6144]{3,2,1,0:T(8,128)(2,1)S(1)} %get-tuple-element.12, bf16[1,2,48,6144]{3,2,1,0:T(8,128)(2,1)S(1)} %get-tuple-element.11), kind=kLoop, calls=%fused_computation | loop fusion | flops 1179648 | bytes 4718592 | tf_op jit(solution)/shard_map/stack | solution.py:371
  62.2 0.0 copy-done.1
  62.2 0.1 select_reduce_fusion.1
  62.4 0.0 copy-done
  62.4 0.9 %pad_maximum_fusion.1 = bf16[2,2,48,1536]{3,2,1,0:T(8,128)(2,1)} fusion(bf16[1,2,48,1536]{3,2,1,0:T(8,128)(2,1)S(1)} %get-tuple-element.14, bf16[1,2,48,1536]{3,2,1,0:T(8,128)(2,1)S(1)} %get-tuple-element.13), kind=kLoop, calls=%fused_computation.3 | loop fusion | flops 294912 | bytes 1179648 | tf_op jit(solution)/shard_map/stack | solution.py:371
  63.3 0.6 %reshape.59 = f32[192]{0:T(256)} reshape(f32[2,2,48]{2,1,0:T(2,128)S(1)} %pad_maximum_fusion.2) | data formatting | bytes 1536 | tf_op jit(solution)/shard_map/reshape | solution.py:371
  (2 shorter events, 0.0 us)
Async XLA Ops:
  60.6 1.6 %copy-start.1 = (f32[2,2,48,128]{3,2,1,0:T(8,128)S(1)}, f32[2,2,48,128]{3,2,1,0:T(8,128)}, u32[]{:S(2)}) copy-start(f32[2,2,48,128]{3,2,1,0:T(8,128)} %get-tuple-element.7) | copy-start | bytes 294916
  60.6 1.7 %copy-start = (bf16[2,2,48,1536]{3,2,1,0:T(8,128)(2,1)S(1)}, bf16[2,2,48,1536]{3,2,1,0:T(8,128)(2,1)}, u32[]{:S(2)}) copy-start(bf16[2,2,48,1536]{3,2,1,0:T(8,128)(2,1)} %get-tuple-element.8) | copy-start | bytes 1769476
